TPU v7x, 256 devices: a 8x8x2 block of a 8x8x16 slice. The times are simulated.
256 devices in a mesh: grp: 2 (over z), kvp: 16 (over x, core), tp: 8 (over y).
Axes of the slice: x: 8, y: 8, z: 2, core: 2. Of those that a mesh axis runs over, the one named last changes fastest.
The devices are a block of a 8x8x16 slice.
Arguments:
- hidden_in: bfloat16 [16, 7168], P('grp'), parts along dimension 0, may hold values from -3 to 3
- queries_nope: bfloat16 [16, 128, 128], P('grp', ('kvp', 'tp')), parts along dimension 0, may hold values from -6 to 6
- queries_rope: bfloat16 [16, 128, 64], P('grp', ('kvp', 'tp')), parts along dimension 0, may hold values from -26 to 26
- cache: bfloat16 [16, 6144, 576], P('grp', 'kvp'), parts along dimension 0, may hold values from -20 to 20
- lengths: int32 [16], P('grp'), parts along dimension 0, may hold values from 128 to 6144, as said below
- w_uk: bfloat16 [128, 128, 512], P(('kvp', 'tp')), may hold values from -0.5 to 0.5
- w_uv: bfloat16 [128, 512, 128], P(('kvp', 'tp')), may hold values from -0.25 to 0.25
- w_out: bfloat16 [16384, 7168], P(('kvp', 'tp')), may hold values from -0.1875 to 0.1875
- norm_gain: float32 [7168], replicated, may hold values from 0.25 to 1.75
- w_gate: bfloat16 [7168, 18432], P(None, ('kvp', 'tp')), may hold values from -0.0625 to 0.0625
- w_up: bfloat16 [7168, 18432], P(None, ('kvp', 'tp')), may hold values from -0.0625 to 0.0625
- w_down: bfloat16 [18432, 7168], P(('kvp', 'tp')), may hold values from -0.15625 to 0.15625
Outputs:
- layer_out: bfloat16 [16, 7168], P('grp', ('kvp', 'tp')), parts along dimension 0
There are 2 independent parts, one for each index of `grp`. A program takes and returns all parts, laid end to end along the dimension named above; an argument that names none is the same for every part. Nothing has to cross between parts.
Inputs may be any that keep to these rules, and one draw needn't show every extreme that they name: `lengths`: every length is a multiple of 128; in every draw some request has the full 6144.
All inputs are finite; a program needn't handle non-finite values.
Results may differ from a plain program's by a relative error of at most 0.04.
Values may be sent and summed in bfloat16 or wider, within the bound.
No kernel may reach another device: no remote copies, remote signals or barrier semaphores. Data moves between devices by JAX's collectives and lax.ppermute only.
A program may use at most 64 MiB of HBM per device.

v0:
```python
import jax
import jax.numpy as jnp
from jax import lax
from jax.sharding import Mesh
from jax.sharding import PartitionSpec as P

KVP = ("kvp_0", "kvp_1")
KVP_TP = ("kvp_0", "kvp_1", "tp")


def in_one_piece(arrays, axis, dim, along):
    both = jnp.concatenate(arrays, axis=along)
    whole, at, gathered = (lax.all_gather(both, axis, axis=dim, tiled=True), 0, [])
    for a in arrays:
        gathered.append(lax.slice_in_dim(whole, at, at + a.shape[along], axis=along))
        at += a.shape[along]
    return tuple(gathered)


def sum_in_order(blocks, axes, sequence):
    inside = blocks.shape[1:]
    blocks = blocks.reshape(*(lax.axis_size(a) for a in axes), *inside)
    blocks = jnp.moveaxis(blocks, sequence, range(len(axes))).reshape(-1, *inside)
    for k in sequence:
        blocks = lax.psum_scatter(blocks, axes[k], scatter_dimension=0, tiled=True)
    return blocks[0]


def in_blocks(value, dim, size):
    dims = value.shape
    blocks = value.reshape(*dims[:dim], size, dims[dim] // size, *dims[dim + 1 :])
    return jnp.moveaxis(blocks, dim, 0)


def sum_by_axis(value, axes, sequence, dim):
    size = lax.axis_size(axes)
    return sum_in_order(in_blocks(value, dim, size), axes, sequence)


def project(o_lat, w_uv, w_out):
    head_out = jnp.einsum("bhl,hle->bhe", o_lat, w_uv, preferred_element_type=jnp.float32).astype(
        jnp.bfloat16
    )
    return jnp.dot(
        head_out.reshape(head_out.shape[0], -1), w_out, preferred_element_type=jnp.float32
    )


def per_device(
    hidden_in,
    queries_nope,
    queries_rope,
    cache,
    lengths,
    w_uk,
    w_uv,
    w_out,
    norm_gain,
    w_gate,
    w_up,
    w_down,
):
    batch, heads_dev, head_dim = queries_nope.shape
    latent = w_uk.shape[2]
    ctx_dev = cache.shape[1]
    groups = lax.axis_size(KVP)
    score_scale = float(head_dim + queries_rope.shape[2]) ** (-0.5)
    q_lat = jnp.einsum(
        "bhd,hdl->bhl", queries_nope, w_uk, preferred_element_type=jnp.float32
    ).astype(jnp.bfloat16)
    q_lat_all, rope_all = in_one_piece((q_lat, queries_rope), KVP, 1, 2)
    q_full = jnp.concatenate([q_lat_all, rope_all], axis=2)
    scores = (
        jnp.einsum("bhc,btc->bht", q_full, cache, preferred_element_type=jnp.float32) * score_scale
    )
    offset = lax.axis_index(KVP) * ctx_dev
    visible = ((offset + jnp.arange(ctx_dev, dtype=jnp.int32))[None, :] < lengths[:, None])[
        :, None, :
    ]
    masked = jnp.where(visible, scores, jnp.float32(-1e30))
    block_max = jnp.max(masked, axis=2)
    exponent = jnp.where(visible, jnp.exp(masked - block_max[..., None]), jnp.float32(0.0))
    guarded = jnp.maximum(jnp.sum(exponent, axis=2), 1.0)
    log_total = block_max + jnp.log(guarded)
    weights = (exponent / guarded[..., None]).astype(jnp.bfloat16)
    partial_value = jnp.einsum("bht,btc->bhc", weights, cache, preferred_element_type=jnp.float32)[
        ..., :latent
    ]
    blocks = partial_value.reshape(batch, groups, heads_dev, latent)
    block_logs = log_total.reshape(batch, groups, heads_dev)
    part_blocks = lax.all_to_all(
        blocks.astype(jnp.bfloat16), KVP, split_axis=1, concat_axis=1, tiled=True
    ).astype(blocks.dtype)
    part_logs = lax.all_to_all(
        block_logs.astype(jnp.bfloat16), KVP, split_axis=1, concat_axis=1, tiled=True
    ).astype(block_logs.dtype)
    highest = jnp.max(part_logs, axis=1)
    overall = highest + jnp.log(jnp.sum(jnp.exp(part_logs - highest[:, None, :]), axis=1))
    scaled = jnp.exp(part_logs - overall[:, None, :])[..., None] * part_blocks
    o_lat = jnp.sum(scaled, axis=1).astype(jnp.bfloat16)
    attention = project(o_lat, w_uv, w_out)
    model_width = norm_gain.shape[0]
    share_width = model_width // lax.axis_size(KVP_TP)
    share_start = lax.axis_index(KVP_TP) * share_width
    attn_whole = lax.psum(attention, KVP_TP)
    residual = hidden_in.astype(jnp.float32) + attn_whole
    mean_square = jnp.mean(residual * residual, axis=1)
    normed = (residual * lax.rsqrt(mean_square + 1e-06)[:, None] * norm_gain[None, :]).astype(
        jnp.bfloat16
    )
    residual_share = lax.dynamic_slice_in_dim(residual, share_start, share_width, 1)
    gate_proj = jnp.dot(normed, w_gate, preferred_element_type=jnp.float32)
    up_proj = jnp.dot(normed, w_up, preferred_element_type=jnp.float32)
    act = (jax.nn.silu(gate_proj) * up_proj).astype(jnp.bfloat16)
    ffn_terms = jnp.dot(act, w_down, preferred_element_type=jnp.float32)
    ffn_share = sum_by_axis(ffn_terms, KVP_TP, (1, 0, 2), 1)
    return (residual_share + ffn_share).astype(jnp.bfloat16)


def solution(mesh):
    torus = Mesh(
        mesh.devices.reshape(mesh.shape["grp"], 8, 2, mesh.shape["tp"]),
        ("grp", "kvp_0", "kvp_1", "tp"),
    )
    return jax.shard_map(
        per_device,
        mesh=torus,
        in_specs=(
            P("grp", None),
            P("grp", KVP_TP, None),
            P("grp", KVP_TP, None),
            P("grp", KVP, None),
            P("grp"),
            P(KVP_TP, None, None),
            P(KVP_TP, None, None),
            P(KVP_TP, None),
            P(),
            P(None, KVP_TP),
            P(None, KVP_TP),
            P(KVP_TP, None),
        ),
        out_specs=P("grp", KVP_TP),
        check_vma=False,
    )
```

profile of v0, /device:TPU:514, one launch (start us, length us, event | category | flops | bytes accessed | tf_op | source)
XLA Modules:
  0.0 365.7 jit_solution(1368219524394948218)
XLA Ops:
  6.6 1.2 fusion.1
  7.7 0.7 pad_maximum_fusion
  8.4 34.0 %all_gather.3 = bf16[8,16,576]{2,0,1:T(8,128)(2,1)S(1)} all-gather(bf16[8,1,576]{2,0,1:T(8,128)(2,1)S(1)} %pad_maximum_fusion), channel_id=1, replica_groups=mesh['grp'=2,'kvp_0'=8,'kvp_1'=2,'tp'=8] {'kvp_0','kvp_1'}, dimensions={1}, use_global_device_ids=true | all-gather | bytes 156672 | tf_op jit(solution)/shard_map/all_gather | solution.py:13
  42.4 0.7 broadcast_compare_fusion
  43.1 0.7 fusion.35
  43.8 0.7 copy-done.2
  44.5 0.2 fusion.6
  44.7 0.6 fusion.30
  45.3 0.7 copy.24
  45.9 3.6 all-to-all-start
  49.5 2.0 fusion.11
  51.6 0.7 copy.27
  52.3 3.4 all-to-all-done
  55.7 5.4 %all-to-all-start.1 = ((bf16[8,16,1,512]{3,0,2,1:T(8,128)(2,1)}), bf16[8,16,1,512]{3,0,2,1:T(8,128)(2,1)}, u32[]{:S(2)}, u32[]{:S(2)}) async-start(bf16[8,16,1,512]{3,0,2,1:T(8,128)(2,1)} %copy.27), calls=%async_computation.1 | async-start | bytes 262144 | tf_op jit(solution)/shard_map/all_to_all | solution.py:91
  61.2 0.5 reduce_max.25
  61.7 0.1 copy.25
  61.8 0.8 fusion.24
  62.8 5.9 %all-to-all-done.1 = bf16[8,16,1,512]{3,0,2,1:T(8,128)(2,1)} async-done(((bf16[8,16,1,512]{3,0,2,1:T(8,128)(2,1)}), bf16[8,16,1,512]{3,0,2,1:T(8,128)(2,1)}, u32[]{:S(2)}, u32[]{:S(2)}) %all-to-all-start.1) | async-done | bytes 131104 | tf_op jit(solution)/shard_map/all_to_all | solution.py:91
  68.7 1.0 multiply_reduce_fusion
  69.7 2.7 fusion.4
  72.5 185.7 %all-reduce.3.cloned.1.call-done = f32[8,7168]{1,0:T(8,128)} async-done(((f32[8,7168]{1,0:T(8,128)}), f32[8,7168]{1,0:T(8,128)}) %all-reduce.3.cloned.1.call-update) | async-done | bytes 229392 | tf_op jit(solution)/shard_map/psum | solution.py:105
  258.3 1.2 multiply_reduce_fusion.1
  259.5 0.7 copy-done.1
  260.2 2.3 fusion.34
  262.4 4.6 %fusion.3 = f32[8,7168]{1,0:T(8,128)} fusion(bf16[144,7168]{1,0:T(8,128)(2,1)} %param.23, bf16[7168,144]{0,1:T(8,128)(2,1)} %param.22, f32[8,144]{1,0:T(8,128)S(1)} %fusion.34, f32[8,7168]{1,0:T(8,128)} %copy-done.1, f32[7168]{0:T(1024)} %param.20, f32[8]{0:T(128)S(1)} %add_rsqrt_fusion), kind=kOutput, calls=%fused_computation.6 | convolution fusion | flops 33209088 | bytes 4620832 | tf_op jit(solution)/shard_map/dot_general | solution.py:115
  267.1 2.2 reshape.125
  269.3 2.2 copy.29
  271.5 12.6 %reduce-scatter.3.cloned.1.call-done = f32[64,8,56]{2,1,0:T(8,128)} async-done(((f32[128,8,56]{2,1,0:T(8,128)}), f32[64,8,56]{2,1,0:T(8,128)}) %reduce-scatter.3.cloned.1.call-update) | async-done | bytes 114704 | tf_op jit(solution)/shard_map/reduce_scatter | solution.py:25
  284.3 0.6 dynamic-slice
  284.8 41.0 %reduce-scatter.5.cloned.1.call-done = f32[8,8,56]{2,1,0:T(8,128)} async-done(((f32[64,8,56]{2,1,0:T(8,128)}), f32[8,8,56]{2,1,0:T(8,128)}) %reduce-scatter.5.cloned.1.call-update) | async-done | bytes 14352 | tf_op jit(solution)/shard_map/reduce_scatter | solution.py:25
  325.8 31.4 %all-reduce = f32[8,8,56]{2,1,0:T(8,128)} all-reduce(f32[8,8,56]{2,1,0:T(8,128)} %reduce-scatter.5.cloned.1.call-done), channel_id=4, replica_groups=mesh['grp'=2,'kvp_0'=8,'kvp_1'=2,'tp'=8] {'tp'}, use_global_device_ids=true, to_apply=%region_9.10.clone | all-reduce | flops 3584 | bytes 28672
  357.3 1.9 fusion.28
  (19 shorter events, 0.6 us)
Async XLA Ops:
  6.5 36.6 %copy-start = (bf16[8,384,576]{1,2,0:T(8,128)(2,1)S(1)}, bf16[8,384,576]{1,2,0:T(8,128)(2,1)}, u32[]{:S(2)}) copy-start(bf16[8,384,576]{1,2,0:T(8,128)(2,1)} %param.15) | copy-start | bytes 10616836
  43.8 0.7 copy-start.2
  45.9 9.8 %all-to-all-start = ((bf16[8,16,1]{0,2,1:T(2,128)(2,1)}), bf16[8,16,1]{0,2,1:T(2,128)(2,1)S(1)}, u32[]{:S(2)}, u32[]{:S(2)}) async-start(bf16[8,16,1]{0,2,1:T(2,128)(2,1)} %copy.24), calls=%async_computation | async-start | bytes 16384 | tf_op jit(solution)/shard_map/all_to_all | solution.py:94
  55.7 12.9 %all-to-all-start.1 = ((bf16[8,16,1,512]{3,0,2,1:T(8,128)(2,1)}), bf16[8,16,1,512]{3,0,2,1:T(8,128)(2,1)}, u32[]{:S(2)}, u32[]{:S(2)}) async-start(bf16[8,16,1,512]{3,0,2,1:T(8,128)(2,1)} %copy.27), calls=%async_computation.1 | async-start | bytes 262144 | tf_op jit(solution)/shard_map/all_to_all | solution.py:91
  61.1 197.2 %all-reduce.3.cloned.1.call-start = ((), (), s32[]{:S(2)}) async-start(), calls=%async_computation.4 | async-start | bytes 458752 | tf_op jit(solution)/shard_map/psum | solution.py:105
  72.5 211.7 %reduce-scatter.3.cloned.1.call-start = ((), (), s32[]{:S(2)}) async-start(), calls=%async_computation.5 | async-start | bytes 786432 | tf_op jit(solution)/shard_map/reduce_scatter | solution.py:25
  259.5 0.7 copy-start.1
  267.1 17.2 %copy-start.3 = (u32[256]{0:T(256)S(1)}, u32[256]{0:T(256)}, u32[]{:S(2)}) copy-start(u32[256]{0:T(256)} %constant.55) | copy-start | bytes 3076
  271.5 54.4 %reduce-scatter.5.cloned.1.call-start = ((), (), s32[]{:S(2)}) async-start(), calls=%async_computation.6 | async-start | bytes 294912 | tf_op jit(solution)/shard_map/reduce_scatter | solution.py:25
Sparse Core Ops, SparseCore 0:
  72.6 185.6 all-reduce.2
  271.6 12.5 reduce-scatter.2
  286.7 39.0 reduce-scatter.4
where the time goes:
time: 366 us
  waiting for transfers between devices  249 us (68%)
  blocking collectives  65.4 us (18%)
  matrix products  13.5 us (4%)
  between operations  13.2 us (4%)
  starting transfers between devices  9.14 us (2%)
  local copies, waits for them, and re-layouts  7.86 us (2%)
  other arithmetic  7.76 us (2%)
    psum x1, waiting for transfers between devices, per_device(): attn_whole = lax.psum(attention, KVP_TP)  186 us
    reduce_scatter x2, waiting for transfers between devices, sum_in_order(): blocks = lax.psum_scatter(blocks, axes[k], scatter_dimension=0, tiled=True)  53.6 us
    all_gather x1, blocking collectives, in_one_piece(): lax.all_gather(both, axis, axis=dim, tiled=True)  34 us
    unnamed x1, blocking collectives  31.4 us
  transfers between devices with their start and end apart: 5, of which 5 were waited for; matrix products, arithmetic and copies ran while one was open for 1% of the time, Pallas kernels for 0%

commit v1 on v0

v1 whole, which is shorter than its diff:
```python
import jax
import jax.numpy as jnp
from jax import lax
from jax.sharding import Mesh
from jax.sharding import PartitionSpec as P

KVP = ("kvp_0", "kvp_1")
KVP_TP = ("kvp_0", "kvp_1", "tp")
F32 = jnp.float32
BF16 = jnp.bfloat16


def exchange(blocks, axes):
    return lax.all_to_all(blocks, axes, split_axis=0, concat_axis=0, tiled=True)


def spread(value, axes):
    return exchange(jnp.broadcast_to(value[None], (lax.axis_size(axes), *value.shape)), axes)


def in_blocks(value, size):
    rows, width = value.shape
    return jnp.moveaxis(value.reshape(rows, size, width // size), 1, 0)


def per_device(
    hidden_in,
    queries_nope,
    queries_rope,
    cache,
    lengths,
    w_uk,
    w_uv,
    w_out,
    norm_gain,
    w_gate,
    w_up,
    w_down,
):
    batch, heads_dev, head_dim = queries_nope.shape
    latent = w_uk.shape[2]
    ctx_dev = cache.shape[1]
    groups = lax.axis_size(KVP)
    columns = lax.axis_size("tp")
    score_scale = float(head_dim + queries_rope.shape[2]) ** (-0.5)
    q_lat = jnp.dot(queries_nope[:, 0], w_uk[0], preferred_element_type=F32).astype(BF16)
    q_full = spread(jnp.concatenate([q_lat, queries_rope[:, 0]], axis=1), KVP)
    scores = jnp.einsum("hbc,btc->bht", q_full, cache, preferred_element_type=F32) * score_scale
    offset = lax.axis_index(KVP) * ctx_dev
    visible = ((offset + jnp.arange(ctx_dev, dtype=jnp.int32))[None, :] < lengths[:, None])[
        :, None, :
    ]
    masked = jnp.where(visible, scores, F32(-1e30))
    block_max = jnp.max(masked, axis=2)
    exponent = jnp.where(visible, jnp.exp(masked - block_max[..., None]), F32(0.0))
    guarded = jnp.maximum(jnp.sum(exponent, axis=2), 1.0)
    log_total = block_max + jnp.log(guarded)
    weights = (exponent / guarded[..., None]).astype(BF16)
    partial_value = jnp.einsum("bht,btc->hbc", weights, cache, preferred_element_type=F32)[
        ..., :latent
    ]
    logs = log_total.T[..., None]
    high = lax.reduce_precision(logs, 8, 7)
    low = logs - high
    lane = lax.broadcasted_iota(jnp.int32, (1, 1, 128), 2)
    tail = jnp.where(lane == 0, high, jnp.where(lane == 1, low, F32(0.0)))
    parts = exchange(jnp.concatenate([partial_value, tail], axis=2).astype(BF16), KVP)
    part_logs = parts[..., latent].astype(F32) + parts[..., latent + 1].astype(F32)
    highest = jnp.max(part_logs, axis=0)
    overall = highest + jnp.log(jnp.sum(jnp.exp(part_logs - highest[None]), axis=0))
    share = jnp.exp(part_logs - overall[None])[..., None]
    o_lat = jnp.sum(share * parts[..., :latent].astype(F32), axis=0).astype(BF16)
    head_out = jnp.dot(o_lat, w_uv[0], preferred_element_type=F32).astype(BF16)
    attention = jnp.dot(head_out, w_out, preferred_element_type=F32).astype(BF16)

    slab = jnp.sum(exchange(in_blocks(attention, groups), KVP).astype(F32), axis=0)
    slab = jnp.sum(spread(slab.astype(BF16), "tp").astype(F32), axis=0)
    slab_width = slab.shape[1]
    share_width = slab_width // columns
    hidden_slab = lax.dynamic_slice_in_dim(
        hidden_in, lax.axis_index(KVP) * slab_width, slab_width, 1
    )
    slab = slab + hidden_slab.astype(F32)
    residual_share = lax.dynamic_slice_in_dim(
        slab, lax.axis_index("tp") * share_width, share_width, 1
    )
    residual = jnp.moveaxis(spread(slab.astype(BF16), KVP), 0, 1).reshape(batch, -1).astype(F32)
    mean_square = jnp.mean(residual * residual, axis=1)
    normed = (residual * lax.rsqrt(mean_square + 1e-06)[:, None] * norm_gain[None, :]).astype(BF16)
    gate_proj = jnp.dot(normed, w_gate, preferred_element_type=F32)
    up_proj = jnp.dot(normed, w_up, preferred_element_type=F32)
    act = (jax.nn.silu(gate_proj) * up_proj).astype(BF16)
    ffn_terms = jnp.dot(act, w_down, preferred_element_type=F32).astype(BF16)
    ffn_blocks = exchange(in_blocks(ffn_terms, groups * columns), KVP_TP)
    ffn_share = jnp.sum(ffn_blocks.astype(F32), axis=0)
    return (residual_share + ffn_share).astype(BF16)


def solution(mesh):
    torus = Mesh(
        mesh.devices.reshape(
            mesh.shape["grp"], mesh.shape["kvp"] // 2, 2, mesh.shape["tp"]
        ),
        ("grp", "kvp_0", "kvp_1", "tp"),
    )
    return jax.shard_map(
        per_device,
        mesh=torus,
        in_specs=(
            P("grp", None),
            P("grp", KVP_TP, None),
            P("grp", KVP_TP, None),
            P("grp", KVP, None),
            P("grp"),
            P(KVP_TP, None, None),
            P(KVP_TP, None, None),
            P(KVP_TP, None),
            P(),
            P(None, KVP_TP),
            P(None, KVP_TP),
            P(KVP_TP, None),
        ),
        out_specs=P("grp", KVP_TP),
        check_vma=False,
    )
```

time: 366 us -> 144 us (0.39)
  waiting for transfers between devices: 249 us -> 27.1 us
  blocking collectives: 65.4 us -> 36.1 us
  starting transfers between devices: 9.14 us -> 36.8 us
  between operations: 13.2 us -> 0.14 us
  local copies, waits for them, and re-layouts: 7.86 us -> 18.1 us
    psum x1 -> x0, waiting for transfers between devices: 186 us -> none  [per_device(): attn_whole = lax.psum(attention, KVP_TP)]
    reduce_scatter x2 -> x0, waiting for transfers between devices: 53.6 us -> none  [sum_in_order(): blocks = lax.psum_scatter(blocks, axes[k], scatter_dimension=0, tiled=True)]
    all_to_all x0 -> x3, blocking collectives: none -> 36.1 us  [exchange(): return lax.all_to_all(blocks, axes, split_axis=0, concat_axis=0, tiled=True)]
    all_gather x1 -> x0, blocking collectives: 34 us -> none  [in_one_piece(): lax.all_gather(both, axis, axis=dim, tiled=True)]
    unnamed x1 -> x0, blocking collectives: 31.4 us -> none
    all_to_all x2 -> x3, starting transfers between devices: 8.95 us -> 36.8 us  [exchange(): return lax.all_to_all(blocks, axes, split_axis=0, concat_axis=0, tiled=True)]
    all_to_all x2 -> x3, waiting for transfers between devices: 9.32 us -> 27.1 us  [exchange(): return lax.all_to_all(blocks, axes, split_axis=0, concat_axis=0, tiled=True)]
    unnamed x9 -> x8, local copies, waits for them, and re-layouts: 1.94 us -> 6.1 us
  transfers between devices with their start and end apart: 5 -> 3, of which waited for: 5 -> 3; matrix products, arithmetic and copies ran while one was open for 1% -> 1% of each run, Pallas kernels for 0% -> 0%
where the time goes in v1:
time: 144 us; the launch traced here: 141 us
  starting transfers between devices  36.8 us (26%)
  blocking collectives  36.1 us (25%)
  waiting for transfers between devices  27.1 us (19%)
  local copies, waits for them, and re-layouts  18.1 us (13%)
  matrix products  13.5 us (9%)
  other arithmetic  9.56 us (7%)
    all_to_all x3, starting transfers between devices, exchange(): return lax.all_to_all(blocks, axes, split_axis=0, concat_axis=0, tiled=True)  36.8 us
    all_to_all x3, blocking collectives, exchange(): return lax.all_to_all(blocks, axes, split_axis=0, concat_axis=0, tiled=True)  36.1 us
    all_to_all x3, waiting for transfers between devices, exchange(): return lax.all_to_all(blocks, axes, split_axis=0, concat_axis=0, tiled=True)  27.1 us
    unnamed x8, local copies, waits for them, and re-layouts  6.1 us
    reshape x3, local copies, waits for them, and re-layouts, in_blocks(): return jnp.moveaxis(value.reshape(rows, size, width // size), 1, 0)  4.79 us
    dot_general x1, matrix products, per_device(): ffn_terms = jnp.dot(act, w_down, preferred_element_type=F32).astype(BF16)  4.61 us
  transfers between devices with their start and end apart: 3, of which 3 were waited for; matrix products, arithmetic and copies ran while one was open for 1% of the time, Pallas kernels for 0%

profile of v1, /device:TPU:514, one launch (start us, length us, event | category | flops | bytes accessed | tf_op | source)
XLA Modules:
  0.0 141.3 jit_solution(18407414616289436827)
XLA Ops:
  0.0 1.2 convolution_convert_fusion.3
  2.6 23.3 %all-to-all-start = ((bf16[16,8,576]{2,1,0:T(8,128)(2,1)}), bf16[16,8,576]{2,1,0:T(8,128)(2,1)}, u32[]{:S(2)}, u32[]{:S(2)}) async-start(bf16[16,8,576]{2,1,0:T(8,128)(2,1)} %broadcast_in_dim.84), calls=%async_computation | async-start | bytes 327680 | tf_op jit(solution)/shard_map/all_to_all | solution.py:14
  26.6 7.3 %all-to-all-done = bf16[16,8,576]{2,1,0:T(8,128)(2,1)} async-done(((bf16[16,8,576]{2,1,0:T(8,128)(2,1)}), bf16[16,8,576]{2,1,0:T(8,128)(2,1)}, u32[]{:S(2)}, u32[]{:S(2)}) %all-to-all-start) | async-done | bytes 147488 | tf_op jit(solution)/shard_map/all_to_all | solution.py:14
  33.9 1.6 %fusion.30 = (f32[8,16]{1,0:T(8,128)S(1)}, f32[8,16,384]{2,1,0:T(8,128)S(1)}) fusion(bf16[8,384,576]{1,2,0:T(8,128)(2,1)S(1)} %copy-done, bf16[16,8,576]{2,1,0:T(8,128)(2,1)} %all-to-all-done, pred[8,384]{1,0:T(8,128)(4,1)S(1)} %broadcast_compare_fusion), kind=kOutput, calls=%fused_computation.62 | convolution fusion | flops 56770432 | bytes 3886592 | tf_op jit(solution)/shard_map/hbc,btc->bht/dot_general | solution.py:48
  35.7 1.1 fusion.1
  37.0 12.2 %all_to_all.30 = bf16[16,8,640]{2,1,0:T(8,128)(2,1)S(1)} all-to-all(bf16[16,8,640]{2,1,0:T(8,128)(2,1)S(1)} %copy.22), channel_id=1, replica_groups=mesh['grp'=2,'kvp_0'=8,'kvp_1'=2,'tp'=8] {'kvp_0','kvp_1'}, dimensions={0} | all-to-all | bytes 327680 | tf_op jit(solution)/shard_map/all_to_all | solution.py:14
  50.6 0.9 copy.29
  51.5 0.9 copy.30
  53.4 0.7 copy.25
  54.1 1.0 multiply_reduce_fusion
  55.1 2.7 %convolution_convert_fusion.1 = bf16[8,7168]{1,0:T(8,128)(2,1)} fusion(bf16[128,7168]{1,0:T(8,128)(2,1)} %param.19, bf16[1,512,128]{2,1,0:T(8,128)(2,1)} %param.18, bf16[8,512]{1,0:T(8,128)(2,1)S(1)} %multiply_reduce_fusion), kind=kOutput, calls=%fused_computation.1 | convolution fusion | flops 15787008 | bytes 2088960 | tf_op jit(solution)/shard_map/dot_general | solution.py:74
  57.8 1.7 %reshape.80 = bf16[8,16,448]{2,1,0:T(8,128)(2,1)} reshape(bf16[8,7168]{1,0:T(8,128)(2,1)} %convolution_convert_fusion.1) | data formatting | bytes 229376 | tf_op jit(solution)/shard_map/reshape | solution.py:23
  59.5 1.0 copy.36
  60.5 12.1 %all_to_all.31 = bf16[16,8,448]{2,1,0:T(8,128)(2,1)} all-to-all(bf16[16,8,448]{2,1,0:T(8,128)(2,1)S(1)} %bitcast.40), channel_id=1, replica_groups=mesh['grp'=2,'kvp_0'=8,'kvp_1'=2,'tp'=8] {'kvp_0','kvp_1'}, dimensions={0} | all-to-all | bytes 229376 | tf_op jit(solution)/shard_map/all_to_all | solution.py:14
  72.6 0.9 reduce_sum.69
  74.2 4.2 %all-to-all-start.3 = ((bf16[8,8,448]{2,1,0:T(8,128)(2,1)}), bf16[8,8,448]{2,1,0:T(8,128)(2,1)}, u32[]{:S(2)}, u32[]{:S(2)}) async-start(bf16[8,8,448]{2,1,0:T(8,128)(2,1)} %broadcast_in_dim.92), calls=%async_computation.3 | async-start | bytes 131072 | tf_op jit(solution)/shard_map/all_to_all | solution.py:14
  78.3 8.4 %all-to-all-done.3 = bf16[8,8,448]{2,1,0:T(8,128)(2,1)} async-done(((bf16[8,8,448]{2,1,0:T(8,128)(2,1)}), bf16[8,8,448]{2,1,0:T(8,128)(2,1)}, u32[]{:S(2)}, u32[]{:S(2)}) %all-to-all-start.3) | async-done | bytes 57376 | tf_op jit(solution)/shard_map/all_to_all | solution.py:14
  86.8 0.9 convert_reduce_fusion.1
  87.6 1.4 fusion.28
  89.0 11.7 %all_to_all.32 = bf16[16,8,448]{2,1,0:T(8,128)(2,1)S(1)} all-to-all(bf16[16,8,448]{2,1,0:T(8,128)(2,1)S(1)} %broadcast_in_dim.93), channel_id=1, replica_groups=mesh['grp'=2,'kvp_0'=8,'kvp_1'=2,'tp'=8] {'kvp_0','kvp_1'}, dimensions={0} | all-to-all | bytes 229376 | tf_op jit(solution)/shard_map/all_to_all | solution.py:14
  101.0 0.9 copy.27
  101.8 1.8 %reshape.82 = f32[8,7168]{1,0:T(8,128)} reshape(f32[8,16,448]{2,1,0:T(8,128)} %copy.27) | data formatting | bytes 458752 | tf_op jit(solution)/shard_map/convert_element_type | solution.py:87
  103.6 2.4 %fusion.27 = f32[8,144]{1,0:T(8,128)S(1)} fusion(bf16[7168,144]{0,1:T(8,128)(2,1)} %param.21, f32[8,7168]{1,0:T(8,128)} %reshape.82, f32[7168]{0:T(1024)} %param.20, f32[8]{0:T(128)S(1)} %add_rsqrt_fusion), kind=kOutput, calls=%fused_computation.59 | convolution fusion | flops 16687104 | bytes 2327072 | tf_op jit(solution)/shard_map/dot_general | solution.py:90
  106.0 4.6 %convolution_convert_fusion = bf16[8,7168]{1,0:T(8,128)(2,1)} fusion(bf16[144,7168]{1,0:T(8,128)(2,1)} %param.23, bf16[7168,144]{0,1:T(8,128)(2,1)} %param.22, f32[8,144]{1,0:T(8,128)S(1)} %fusion.27, f32[8,7168]{1,0:T(8,128)} %reshape.82, f32[7168]{0:T(1024)} %param.20, f32[8]{0:T(128)S(1)} %add_rsqrt_fusion), kind=kOutput, calls=%fused_computation | convolution fusion | flops 33266432 | bytes 4506144 | tf_op jit(solution)/shard_map/dot_general | solution.py:93
  110.6 2.1 %reshape.81 = bf16[8,128,56]{2,1,0:T(8,128)(2,1)} reshape(bf16[8,7168]{1,0:T(8,128)(2,1)} %convolution_convert_fusion) | data formatting | bytes 229376 | tf_op jit(solution)/shard_map/reshape | solution.py:23
  112.7 1.8 %copy.28 = bf16[128,8,56]{2,1,0:T(8,128)(2,1)} copy(bf16[128,8,56]{2,0,1:T(8,128)(2,1)} %bitcast.39) | data formatting | bytes 229376 | tf_op jit(solution)/shard_map/transpose | solution.py:23
  114.5 1.8 %reshape.83 = bf16[128,2,224]{2,1,0:T(2,128)(2,1)} reshape(bf16[128,8,56]{2,1,0:T(8,128)(2,1)} %copy.28) | data formatting | bytes 229376
  116.4 9.3 %all-to-all-start.5 = ((bf16[128,2,224]{2,1,0:T(2,128)(2,1)}), bf16[128,2,224]{2,1,0:T(2,128)(2,1)}, u32[]{:S(2)}, u32[]{:S(2)}) async-start(bf16[128,2,224]{2,1,0:T(2,128)(2,1)} %reshape.83), calls=%async_computation.5 | async-start | bytes 262144 | tf_op jit(solution)/shard_map/all_to_all | solution.py:14
  125.7 11.4 %all-to-all-done.5 = bf16[128,2,224]{2,1,0:T(2,128)(2,1)} async-done(((bf16[128,2,224]{2,1,0:T(2,128)(2,1)}), bf16[128,2,224]{2,1,0:T(2,128)(2,1)}, u32[]{:S(2)}, u32[]{:S(2)}) %all-to-all-start.5) | async-done | bytes 114720 | tf_op jit(solution)/shard_map/all_to_all | solution.py:14
  137.1 1.8 %reshape.84 = bf16[128,8,56]{2,1,0:T(8,128)(2,1)} reshape(bf16[128,2,224]{2,1,0:T(2,128)(2,1)} %all-to-all-done.5) | data formatting | bytes 229376
  138.9 1.1 convert_reduce_fusion
  140.0 1.4 add_convert_fusion
  (26 shorter events, 5.7 us)
Async XLA Ops:
  0.0 33.9 %copy-start = (bf16[8,384,576]{1,2,0:T(8,128)(2,1)S(1)}, bf16[8,384,576]{1,2,0:T(8,128)(2,1)}, u32[]{:S(2)}) copy-start(bf16[8,384,576]{1,2,0:T(8,128)(2,1)} %param.15) | copy-start | bytes 10616836
  2.6 31.4 %all-to-all-start = ((bf16[16,8,576]{2,1,0:T(8,128)(2,1)}), bf16[16,8,576]{2,1,0:T(8,128)(2,1)}, u32[]{:S(2)}, u32[]{:S(2)}) async-start(bf16[16,8,576]{2,1,0:T(8,128)(2,1)} %broadcast_in_dim.84), calls=%async_computation | async-start | bytes 327680 | tf_op jit(solution)/shard_map/all_to_all | solution.py:14
  49.2 0.7 copy-start.1
  74.2 12.6 %all-to-all-start.3 = ((bf16[8,8,448]{2,1,0:T(8,128)(2,1)}), bf16[8,8,448]{2,1,0:T(8,128)(2,1)}, u32[]{:S(2)}, u32[]{:S(2)}) async-start(bf16[8,8,448]{2,1,0:T(8,128)(2,1)} %broadcast_in_dim.92), calls=%async_computation.3 | async-start | bytes 131072 | tf_op jit(solution)/shard_map/all_to_all | solution.py:14
  116.4 20.7 %all-to-all-start.5 = ((bf16[128,2,224]{2,1,0:T(2,128)(2,1)}), bf16[128,2,224]{2,1,0:T(2,128)(2,1)}, u32[]{:S(2)}, u32[]{:S(2)}) async-start(bf16[128,2,224]{2,1,0:T(2,128)(2,1)} %reshape.83), calls=%async_computation.5 | async-start | bytes 262144 | tf_op jit(solution)/shard_map/all_to_all | solution.py:14

commit v2 on v1

v2 whole, which is shorter than its diff:
```python
import functools

import jax
import jax.numpy as jnp
from jax import lax
from jax.experimental import pallas as pl
from jax.experimental.pallas import tpu as pltpu
from jax.sharding import Mesh
from jax.sharding import PartitionSpec as P

KVP = ("kvp_0", "kvp_1")
KVP_TP = ("kvp_0", "kvp_1", "tp")
F32 = jnp.float32
BF16 = jnp.bfloat16
LANES = 128
OUT_CHUNKS = 4
OUT_GRANT = 3 << 20
FFN_GRANT = 8 << 20
VMEM = pl.BlockSpec(memory_space=pltpu.VMEM)
HBM = pl.BlockSpec(memory_space=pltpu.HBM)


def exchange(blocks, axes):
    return lax.all_to_all(blocks, axes, split_axis=0, concat_axis=0, tiled=True)


def call(body, outs, specs, *operands, scratch=(), grant=2 << 20):
    return pl.pallas_call(
        body,
        out_shape=outs,
        in_specs=specs,
        out_specs=[VMEM] * len(outs),
        scratch_shapes=scratch,
        compiler_params=pltpu.CompilerParams(vmem_limit_bytes=grant),
    )(*operands)


def stay(array):
    return pltpu.with_memory_space_constraint(array, pltpu.HBM)


def columns_of(source, target, sems, first, count):
    width = source.shape[1] // count
    copies = []
    for i in range(count):
        part = (slice(None), pl.ds(i * width, width))
        copies.append(
            pltpu.make_async_copy(source.at[part], target.at[part], sems.at[first + i])
        )
    return copies


def query_kernel(nope, rope, w_uk, out):
    q_lat = jnp.dot(nope[...], w_uk[...], preferred_element_type=F32).astype(BF16)
    latent = q_lat.shape[1]
    for k in range(out.shape[0]):
        out[k, :, :latent] = q_lat
        out[k, :, latent:] = rope[...]


def project_kernel(parts, w_uv, w_out, out, value, rows, sems):
    groups, batch, width = parts.shape
    latent = width - LANES
    first = pltpu.make_async_copy(w_uv, value, sems.at[0])
    chunks = columns_of(w_out, rows, sems, 1, OUT_CHUNKS)
    for copy in (first, *chunks):
        copy.start()
    tail = parts[:, :, latent:].astype(F32)
    logs = tail + pltpu.roll(tail, LANES // 2, 2)
    highest = jnp.max(logs, axis=0)
    overall = highest + jnp.log(jnp.sum(jnp.exp(logs - highest[None]), axis=0))
    share = jnp.exp(logs - overall[None])
    pieces = []
    for at in range(0, latent, LANES):
        piece = jnp.sum(share * parts[:, :, at : at + LANES].astype(F32), axis=0)
        pieces.append(piece.astype(BF16))
    o_lat = jnp.concatenate(pieces, axis=1)
    first.wait()
    head_out = jnp.dot(o_lat, value[...], preferred_element_type=F32).astype(BF16)
    block = out.shape[2]
    for k in range(0, groups, 2):
        if k % (groups // OUT_CHUNKS) == 0:
            chunks[k // (groups // OUT_CHUNKS)].wait()
        both = jnp.dot(
            head_out, rows[:, k * block : (k + 2) * block], preferred_element_type=F32
        )
        out[k] = both[:, :block].astype(BF16)
        out[k + 1] = both[:, block:].astype(BF16)


def sum_kernel(blocks, out):
    total = jnp.sum(blocks[...].astype(F32), axis=0).astype(BF16)
    for t in range(out.shape[0]):
        out[t] = total


def residual_kernel(blocks, hidden, gain, out, slab):
    batch, block = hidden.shape
    total = jnp.sum(blocks[...].astype(F32), axis=0) + hidden[...]
    slab[...] = total
    square = jnp.sum(total * total, axis=1, keepdims=True)
    high = square.astype(BF16).astype(F32)
    spare = out.shape[2] - block
    lane = lax.broadcasted_iota(jnp.int32, (batch, spare), 1)
    tail = jnp.where(lane < spare // 2, high, square - high)
    message = jnp.concatenate([total * gain[...], tail], axis=1).astype(BF16)
    for j in range(out.shape[0]):
        out[j] = message


def ffn_kernel(blocks, gate, up, down, out, value, gates, ups, downs, sems):
    groups, batch, padded = blocks.shape
    width = gate.shape[1]
    block = width // groups
    spare = padded - block
    gate_in = columns_of(gate, gates, sems, 0, 2)
    up_in = columns_of(up, ups, sems, 2, 2)
    down_in = columns_of(down, downs, sems, 4, 2)
    for copy in (gate_in[0], up_in[0], gate_in[1], up_in[1], down_in[0], down_in[1]):
        copy.start()
    tail = jnp.sum(blocks[:, :, padded - LANES :].astype(F32), axis=0)
    square = (
        tail[:, LANES - spare : LANES - spare + 1]
        + tail[:, LANES - spare // 2 : LANES - spare // 2 + 1]
    )
    scale = lax.rsqrt(square / width + 1e-06)
    for k in range(0, groups, 2):
        both = jnp.concatenate(
            [blocks[k].astype(F32)[:, :block], blocks[k + 1].astype(F32)[:, :block]], axis=1
        )
        value[:, k * block : (k + 2) * block] = both.astype(BF16)
    contract = (((1,), (1,)), ((), ()))
    gate_proj = jnp.zeros((batch, gate.shape[0]), F32)
    up_proj = jnp.zeros((batch, gate.shape[0]), F32)
    for i in range(2):
        half = slice(i * (width // 2), (i + 1) * (width // 2))
        gate_in[i].wait()
        gate_proj += lax.dot_general(
            value[:, half], gates[:, half], contract, preferred_element_type=F32
        )
        up_in[i].wait()
        up_proj += lax.dot_general(
            value[:, half], ups[:, half], contract, preferred_element_type=F32
        )
    gate_proj = gate_proj * scale
    up_proj = up_proj * scale
    act = (gate_proj / (1.0 + jnp.exp(-gate_proj)) * up_proj).astype(BF16)
    pieces = out.shape[0] // groups
    share = block // pieces
    fill = jnp.zeros((batch // 2, LANES - 2 * share), F32)
    for k in range(0, groups, 2):
        if k % (groups // 2) == 0:
            down_in[k // (groups // 2)].wait()
        at = k * block
        both = jnp.dot(act, downs[:, at : at + 2 * block], preferred_element_type=F32)
        for j in range(2 * pieces):
            piece = both[:, j * share : (j + 1) * share]
            packed = jnp.concatenate([piece[: batch // 2], piece[batch // 2 :], fill], axis=1)
            out[k * pieces + j] = packed.astype(BF16)


def final_kernel(blocks, slab, out):
    batch, share = out.shape
    total = jnp.sum(blocks[...].astype(F32), axis=0)
    total = jnp.concatenate([total[:, :share], total[:, share : 2 * share]], axis=0)
    t_here = lax.axis_index("tp")
    own = jnp.zeros((batch, share), F32)
    for t in range(slab.shape[1] // share):
        own = jnp.where(t_here == t, slab[:, t * share : (t + 1) * share], own)
    out[...] = (total + own).astype(BF16)


def per_device(
    hidden_in,
    queries_nope,
    queries_rope,
    cache,
    lengths,
    w_uk,
    w_uv,
    w_out,
    norm_gain,
    w_gate,
    w_up,
    w_down,
):
    batch, heads_dev, head_dim = queries_nope.shape
    latent = w_uk.shape[2]
    rope_dim = queries_rope.shape[2]
    ctx_dev = cache.shape[1]
    model_width = norm_gain.shape[0]
    groups = lax.axis_size(KVP)
    columns = lax.axis_size("tp")
    block = model_width // groups
    share_width = block // columns
    padded = -(-block // LANES) * LANES
    shape = jax.ShapeDtypeStruct
    score_scale = float(head_dim + rope_dim) ** (-0.5)

    (q_blocks,) = call(
        query_kernel,
        [shape((groups, batch, latent + rope_dim), BF16)],
        [VMEM] * 3,
        queries_nope[:, 0],
        queries_rope[:, 0],
        w_uk[0],
        grant=60 << 20,
    )
    q_full = exchange(q_blocks, KVP)
    offset = lax.axis_index(KVP) * ctx_dev
    visible = (offset + jnp.arange(ctx_dev, dtype=jnp.int32))[None, :] < lengths[:, None]
    start = lax.axis_index(KVP) * block
    hidden_slab = lax.dynamic_slice_in_dim(hidden_in, start, block, 1).astype(F32)
    gain_slab = lax.dynamic_slice_in_dim(norm_gain, start, block, 0)
    gain_slab = jnp.broadcast_to(gain_slab[None], hidden_slab.shape)
    visible, hidden_slab, gain_slab = lax.optimization_barrier((visible, hidden_slab, gain_slab))
    visible = visible[:, None, :]
    scores = jnp.einsum("hbc,btc->bht", q_full, cache, preferred_element_type=F32) * score_scale
    masked = jnp.where(visible, scores, F32(-1e30))
    block_max = jnp.max(masked, axis=2)
    exponent = jnp.where(visible, jnp.exp(masked - block_max[..., None]), F32(0.0))
    guarded = jnp.maximum(jnp.sum(exponent, axis=2), 1.0)
    log_total = block_max + jnp.log(guarded)
    weights = (exponent / guarded[..., None]).astype(BF16)
    partial_value = jnp.einsum("bht,btc->hbc", weights, cache, preferred_element_type=F32)[
        ..., :latent
    ]
    logs = log_total.T[..., None]
    high = lax.reduce_precision(logs, 8, 7)
    low = logs - high
    lane = lax.broadcasted_iota(jnp.int32, (1, 1, LANES), 2)
    tail = jnp.where(lane < LANES // 2, high, low)
    parts = exchange(jnp.concatenate([partial_value, tail], axis=2).astype(BF16), KVP)

    (terms,) = call(
        project_kernel,
        [shape((groups, batch, block), BF16)],
        [VMEM, HBM, HBM],
        parts,
        stay(w_uv[0]),
        stay(w_out),
        scratch=[
            pltpu.VMEM(w_uv.shape[1:], BF16),
            pltpu.VMEM(w_out.shape, BF16),
            pltpu.SemaphoreType.DMA((1 + OUT_CHUNKS,)),
        ],
        grant=OUT_GRANT,
    )
    terms = exchange(terms, KVP)
    (sums,) = call(sum_kernel, [shape((columns, batch, block), BF16)], [VMEM], terms)
    sums = exchange(sums, "tp")
    residual, slab = call(
        residual_kernel,
        [shape((groups, batch, padded), BF16), shape((batch, block), F32)],
        [VMEM, VMEM, VMEM],
        sums,
        hidden_slab,
        gain_slab,
    )
    residual = exchange(residual, KVP)
    hidden_dev = w_gate.shape[1]
    (ffn_terms,) = call(
        ffn_kernel,
        [shape((groups * columns, batch // 2, LANES), BF16)],
        [VMEM, HBM, HBM, HBM],
        residual,
        stay(w_gate.T),
        stay(w_up.T),
        stay(w_down),
        scratch=[
            pltpu.VMEM((batch, model_width), BF16),
            pltpu.VMEM((hidden_dev, model_width), BF16),
            pltpu.VMEM((hidden_dev, model_width), BF16),
            pltpu.VMEM((hidden_dev, model_width), BF16),
            pltpu.SemaphoreType.DMA((6,)),
        ],
        grant=FFN_GRANT,
    )
    ffn_terms = exchange(ffn_terms, KVP_TP)
    (out,) = call(
        final_kernel, [shape((batch, share_width), BF16)], [VMEM, VMEM], ffn_terms, slab
    )
    return out


def solution(mesh):
    torus = Mesh(
        mesh.devices.reshape(mesh.shape["grp"], mesh.shape["kvp"] // 2, 2, mesh.shape["tp"]),
        ("grp", "kvp_0", "kvp_1", "tp"),
    )
    return jax.shard_map(
        per_device,
        mesh=torus,
        in_specs=(
            P("grp", None),
            P("grp", KVP_TP, None),
            P("grp", KVP_TP, None),
            P("grp", KVP, None),
            P("grp"),
            P(KVP_TP, None, None),
            P(KVP_TP, None, None),
            P(KVP_TP, None),
            P(),
            P(None, KVP_TP),
            P(None, KVP_TP),
            P(KVP_TP, None),
        ),
        out_specs=P("grp", KVP_TP),
        check_vma=False,
    )
```

time: 144 us -> 119 us (0.83)
  blocking collectives: 36.1 us -> 66.1 us
  waiting for transfers between devices: 27.1 us -> 4.06 us
  starting transfers between devices: 36.8 us -> 23.3 us
  local copies, waits for them, and re-layouts: 18.1 us -> 4.74 us
  matrix products: 13.5 us -> 2.65 us
  Pallas kernels: 0 us -> 10.4 us
  other arithmetic: 9.56 us -> 5.11 us
    all_to_all x3 -> x5, blocking collectives: 36.1 us -> 66.1 us  [exchange(): return lax.all_to_all(blocks, axes, split_axis=0, concat_axis=0, tiled=True)]
    all_to_all x3 -> x1, waiting for transfers between devices: 27.1 us -> 4.06 us  [exchange(): return lax.all_to_all(blocks, axes, split_axis=0, concat_axis=0, tiled=True)]
    all_to_all x3 -> x1, starting transfers between devices: 36.8 us -> 23.3 us  [exchange(): return lax.all_to_all(blocks, axes, split_axis=0, concat_axis=0, tiled=True)]
    dot_general x4 -> x0, matrix products: 10.9 us -> none  [the longest x1 4.61 us: per_device(): ffn_terms = jnp.dot(act, w_down, preferred_element_type=F32).astype(BF16)]
    pallas_call x0 -> x6, Pallas kernels: none -> 10.4 us  [call(): pl.pallas_call(body, out_shape=outs, in_specs=specs, out_specs=[VMEM] * l...]
    unnamed x8 -> x6, local copies, waits for them, and re-layouts: 6.1 us -> 0.01 us
    reshape x3 -> x0, local copies, waits for them, and re-layouts: 4.79 us -> none  [in_blocks(): return jnp.moveaxis(value.reshape(rows, size, width // size), 1, 0)]
    reduce_sum x6 -> x0, other arithmetic: 4.24 us -> none  [the longest x1 1.09 us: per_device(): ffn_share = jnp.sum(ffn_blocks.astype(F32), axis=0)]
  transfers between devices with their start and end apart: 3 -> 1, of which waited for: 3 -> 1; matrix products, arithmetic and copies ran while one was open for 1% -> 3% of each run, Pallas kernels for 0% -> 0%
where the time goes in v2:
time: 119 us; the launch traced here: 116 us
  blocking collectives  66.1 us (56%)
  starting transfers between devices  23.3 us (20%)
  Pallas kernels  10.4 us (9%)
  other arithmetic  5.11 us (4%)
  local copies, waits for them, and re-layouts  4.74 us (4%)
  waiting for transfers between devices  4.06 us (3%)
  matrix products  2.65 us (2%)
    all_to_all x5, blocking collectives, exchange(): return lax.all_to_all(blocks, axes, split_axis=0, concat_axis=0, tiled=True)  66.1 us
    all_to_all x1, starting transfers between devices, exchange(): return lax.all_to_all(blocks, axes, split_axis=0, concat_axis=0, tiled=True)  23.3 us
    pallas_call x6, Pallas kernels, call(): pl.pallas_call(body, out_shape=outs, in_specs=specs, out_specs=[VMEM] * l...  10.4 us
    all_to_all x1, waiting for transfers between devices, exchange(): return lax.all_to_all(blocks, axes, split_axis=0, concat_axis=0, tiled=True)  4.06 us
  transfers between devices with their start and end apart: 1, of which 1 were waited for; matrix products, arithmetic and copies ran while one was open for 3% of the time, Pallas kernels for 0%

profile of v2, /device:TPU:514, one launch (start us, length us, event | category | flops | bytes accessed | tf_op | source)
XLA Modules:
  0.0 116.4 jit_solution(8456745877509478145)
XLA Ops:
  0.0 0.0 copy-start
  0.0 1.9 %shard_map.118 = bf16[16,8,576]{2,1,0:T(8,128)(2,1)} custom-call(bf16[8,128]{1,0:T(8,128)(2,1)} %bitcast.21, bf16[8,64]{1,0:T(8,128)(2,1)} %bitcast.22, bf16[128,512]{1,0:T(8,128)(2,1)} %bitcast.20), custom_call_target="tpu_custom_call" | custom-call | tf_op jit(solution)/shard_map/pallas_call | solution.py:28
  1.9 23.3 %all-to-all-start = ((bf16[16,8,576]{2,1,0:T(8,128)(2,1)}), bf16[16,8,576]{2,1,0:T(8,128)(2,1)}, u32[]{:S(2)}, u32[]{:S(2)}) async-start(bf16[16,8,576]{2,1,0:T(8,128)(2,1)} %shard_map.118), calls=%async_computation | async-start | bytes 327680 | tf_op jit(solution)/shard_map/all_to_all | solution.py:24
  25.2 1.3 %broadcast_compare_fusion = pred[8,384]{1,0:T(8,128)(4,1)} fusion(s32[384]{0:T(512)S(1)} %iota_add_fusion, s32[8]{0:T(128)} %param.16), kind=kLoop, calls=%fused_computation.16 | loop fusion | flops 3072 | bytes 4640 | tf_op jit(solution)/shard_map/lt | solution.py:211
  26.5 0.8 dynamic_slice.7
  27.3 0.8 dynamic-slice_convert_fusion.hidden
  28.1 0.6 broadcast_in_dim.54.gain
  28.7 0.5 iota_compare_fusion
  29.2 4.1 %all-to-all-done = bf16[16,8,576]{2,1,0:T(8,128)(2,1)} async-done(((bf16[16,8,576]{2,1,0:T(8,128)(2,1)}), bf16[16,8,576]{2,1,0:T(8,128)(2,1)}, u32[]{:S(2)}, u32[]{:S(2)}) %all-to-all-start) | async-done | bytes 147488 | tf_op jit(solution)/shard_map/all_to_all | solution.py:24
  33.3 0.0 copy-done
  33.3 0.0 copy-start.2
  33.3 1.6 %fusion.10 = (f32[8,16]{1,0:T(8,128)S(1)}, f32[8,16,384]{2,1,0:T(8,128)S(1)}) fusion(bf16[8,384,576]{1,2,0:T(8,128)(2,1)S(1)} %copy-done, bf16[16,8,576]{2,1,0:T(8,128)(2,1)} %all-to-all-done, pred[8,384]{1,0:T(8,128)(4,1)} %broadcast_compare_fusion), kind=kOutput, calls=%fused_computation.24 | convolution fusion | flops 56770432 | bytes 3886592 | tf_op jit(solution)/shard_map/hbc,btc->bht/dot_general | solution.py:218
  34.9 0.0 copy-done.2
  34.9 0.2 fusion.3
  35.1 0.6 bitcast_reduce-precision_fusion
  35.7 1.1 fusion.4
  36.8 0.7 slice.5
  37.4 1.3 %copy.19 = bf16[16,8]{1,0:T(8,128)(2,1)} copy(bf16[16,8]{0,1:T(8,128)(2,1)} %get-tuple-element.15) | data formatting | bytes 512 | tf_op jit(solution)/shard_map/reduce_precision | solution.py:229
  38.8 1.3 %copy.20 = bf16[16,8]{1,0:T(8,128)(2,1)} copy(bf16[16,8]{0,1:T(8,128)(2,1)} %get-tuple-element.16) | data formatting | bytes 512 | tf_op jit(solution)/shard_map/sub | solution.py:230
  40.1 0.0 copy-start.1
  40.1 0.8 select_convert_fusion
  40.9 0.9 pad_maximum_fusion
  41.8 12.2 %all_to_all.30.parts = bf16[16,8,640]{2,1,0:T(8,128)(2,1)S(1)} all-to-all(bf16[16,8,640]{2,1,0:T(8,128)(2,1)S(1)} %pad_maximum_fusion), channel_id=1, replica_groups=mesh['grp'=2,'kvp_0'=8,'kvp_1'=2,'tp'=8] {'kvp_0','kvp_1'}, dimensions={0} | all-to-all | bytes 327680 | tf_op jit(solution)/shard_map/all_to_all | solution.py:24
  54.1 2.2 %shard_map.119 = bf16[16,8,448]{2,1,0:T(8,128)(2,1)S(1)} custom-call(bf16[16,8,640]{2,1,0:T(8,128)(2,1)S(1)} %all_to_all.30.parts, bf16[512,128]{1,0:T(8,128)(2,1)} %bitcast.19, bf16[128,7168]{1,0:T(8,128)(2,1)} %w_out.1), custom_call_target="tpu_custom_call" | custom-call | tf_op jit(solution)/shard_map/pallas_call | solution.py:28
  56.2 11.9 %all_to_all.31.blocks = bf16[16,8,448]{2,1,0:T(8,128)(2,1)S(1)} all-to-all(bf16[16,8,448]{2,1,0:T(8,128)(2,1)S(1)} %shard_map.119), channel_id=1, replica_groups=mesh['grp'=2,'kvp_0'=8,'kvp_1'=2,'tp'=8] {'kvp_0','kvp_1'}, dimensions={0} | all-to-all | bytes 229376 | tf_op jit(solution)/shard_map/all_to_all | solution.py:24
  68.1 11.1 %all_to_all.32.blocks = bf16[8,8,448]{2,1,0:T(8,128)(2,1)S(1)} all-to-all(bf16[8,8,448]{2,1,0:T(8,128)(2,1)S(1)} %shard_map.120), channel_id=1, replica_groups=mesh['grp'=2,'kvp_0'=8,'kvp_1'=2,'tp'=8] {'tp'}, dimensions={0} | all-to-all | bytes 114688 | tf_op jit(solution)/shard_map/all_to_all | solution.py:24
  79.2 0.0 copy-done.1
  79.2 0.2 shard_map.121
  79.4 11.2 %all_to_all.33.blocks = bf16[16,8,512]{2,1,0:T(8,128)(2,1)S(1)} all-to-all(bf16[16,8,512]{2,1,0:T(8,128)(2,1)S(1)} %get-tuple-element.13), channel_id=1, replica_groups=mesh['grp'=2,'kvp_0'=8,'kvp_1'=2,'tp'=8] {'kvp_0','kvp_1'}, dimensions={0} | all-to-all | bytes 262144 | tf_op jit(solution)/shard_map/all_to_all | solution.py:24
  90.6 5.0 %shard_map.122 = bf16[128,4,128]{2,1,0:T(4,128)(2,1)S(1)} custom-call(bf16[16,8,512]{2,1,0:T(8,128)(2,1)S(1)} %all_to_all.33.blocks, bf16[144,7168]{1,0:T(8,128)(2,1)} %bitcast.16, bf16[144,7168]{1,0:T(8,128)(2,1)} %bitcast.17, bf16[144,7168]{1,0:T(8,128)(2,1)} %down.1), custom_call_target="tpu_custom_call" | custom-call | tf_op jit(solution)/shard_map/pallas_call | solution.py:28
  95.5 19.7 %all_to_all.34.blocks = bf16[128,4,128]{2,1,0:T(4,128)(2,1)S(1)} all-to-all(bf16[128,4,128]{2,1,0:T(4,128)(2,1)S(1)} %shard_map.122), channel_id=1, replica_groups=mesh['grp'=2,'kvp_0'=8,'kvp_1'=2,'tp'=8] {'kvp_0','kvp_1','tp'}, dimensions={0} | all-to-all | bytes 262144 | tf_op jit(solution)/shard_map/all_to_all | solution.py:24
  115.2 1.1 shard_map.123
  (4 shorter events, 0.1 us)
Async XLA Ops:
  0.0 33.3 %copy-start = (bf16[8,384,576]{1,2,0:T(8,128)(2,1)S(1)}, bf16[8,384,576]{1,2,0:T(8,128)(2,1)}, u32[]{:S(2)}) copy-start(bf16[8,384,576]{1,2,0:T(8,128)(2,1)} %param.15) | copy-start | bytes 10616836
  1.9 31.4 %all-to-all-start = ((bf16[16,8,576]{2,1,0:T(8,128)(2,1)}), bf16[16,8,576]{2,1,0:T(8,128)(2,1)}, u32[]{:S(2)}, u32[]{:S(2)}) async-start(bf16[16,8,576]{2,1,0:T(8,128)(2,1)} %shard_map.118), calls=%async_computation | async-start | bytes 327680 | tf_op jit(solution)/shard_map/all_to_all | solution.py:24
  33.3 1.6 %copy-start.2 = (pred[8,384]{1,0:T(8,128)(4,1)S(1)}, pred[8,384]{1,0:T(8,128)(4,1)}, u32[]{:S(2)}) copy-start(pred[8,384]{1,0:T(8,128)(4,1)} %broadcast_compare_fusion) | copy-start | bytes 9220
  40.1 39.1 %copy-start.1 = (f32[8,448]{1,0:T(8,128)S(1)}, f32[8,448]{1,0:T(8,128)}, u32[]{:S(2)}) copy-start(f32[8,448]{1,0:T(8,128)} %broadcast_in_dim.54.gain) | copy-start | bytes 43012
